TPU v7x, 32 devices: a whole 2x2x4 slice. The times are simulated.
32 devices in a mesh: crop: 2 (over x), seq: 2 (over y), res: 8 (over z, core).
Axes of the slice: x: 2, y: 2, z: 4, core: 2. Of those that a mesh axis runs over, the one named last changes fastest.
Arguments:
- aligned_chain_embedding: bfloat16 [128, 32, 256], P(('crop', 'seq'), 'res'), parts along dimension 0, may hold values from -6 to 6
- alignment_mask: int32 [128, 32], P(('crop', 'seq'), 'res'), parts along dimension 0, may hold values from 0 to 1, as said below
- resolved_residue_mask: int32 [64], P('crop'), parts along dimension 0, may hold values 0 or 1
- pairwise_state: bfloat16 [64, 32, 128], P(('crop', 'seq'), 'res'), parts along dimension 0, may hold values from -8 to 8
- combined_projection_matrix: bfloat16 [256, 1024], replicated, may hold values from -0.375 to 0.375
- pair_bias_weight: bfloat16 [128, 8], replicated, may hold values from -8 to 8
- final_projection_matrix: bfloat16 [256, 256], replicated, may hold values from -0.375 to 0.375
- left_right_projection_matrix: bfloat16 [256, 64], replicated, may hold values from -1.5 to 1.5
- outer_mean_weight: bfloat16 [1024, 128], replicated, may hold values from -0.1875 to 0.1875
Outputs:
- alignment_output: bfloat16 [128, 32, 256], P(('crop', 'seq'), 'res'), parts along dimension 0
- pairwise_output: bfloat16 [64, 32, 128], P(('crop', 'seq'), 'res'), parts along dimension 0
There are 2 independent parts, one for each index of `crop`. A program takes and returns all parts, laid end to end along the dimension named above; an argument that names none is the same for every part. Nothing has to cross between parts.
Inputs may be any that keep to these rules, and one draw needn't show every extreme that they name: `alignment_mask`: sequence 0 has no gaps.
All inputs are finite; a program needn't handle non-finite values.
Results may differ from a plain program's by a relative error of at most 0.013.
The roundings to bfloat16 on the way count: a program that leaves them out, or rounds other values in their place, can miss the bound.
Values may be sent and summed in bfloat16 or wider, within the bound.
A program may use at most 64 MiB of HBM per device.

v0:
```python
import math
import jax
import jax.numpy as jnp
from jax import lax
from jax.sharding import PartitionSpec as P

ROW_FEATURES = 256
CZ = 128
HEAD_NUMBER = 8
PER_HEAD_DIM = 32
PROJ_FEATURES = 32
epsilon = 1e-05


def layer_normalize(values):
    values = values.astype(jnp.float32)
    average = jnp.mean(values, axis=-1, keepdims=True)
    centered = values - average
    variance = jnp.mean(centered * centered, axis=-1, keepdims=True)
    return centered * lax.rsqrt(variance + epsilon)


def outer_rows(left_side, right_side, project):
    row_total = left_side.shape[1]
    col_total = right_side.shape[1]
    block_rows = math.gcd(row_total, max(1, 2048 // col_total))

    def outer_block(start):
        product = jnp.einsum(
            "sic,sje->ijce", left_side, right_side, preferred_element_type=jnp.float32
        )
        flattened = product.reshape(block_rows * col_total, PROJ_FEATURES * PROJ_FEATURES)
        return jnp.dot(flattened, project, precision=lax.Precision.HIGHEST).reshape(
            block_rows, col_total, CZ
        )

    starts = jnp.arange(row_total // block_rows, dtype=jnp.int32) * block_rows
    return lax.map(outer_block, starts).reshape(row_total, col_total, CZ)


def per_device(
    aligned_chain_embedding,
    alignment_mask,
    resolved_residue_mask,
    pairwise_state,
    combined_projection_matrix,
    pair_bias_weight,
    final_projection_matrix,
    left_right_projection_matrix,
    outer_mean_weight,
):
    chain_count = aligned_chain_embedding.shape[0]
    amino_count = aligned_chain_embedding.shape[1]
    res_ranks = lax.axis_size("res")
    seq_groups = lax.axis_size("seq")
    full_length = amino_count * res_ranks
    row_count = full_length // seq_groups
    item_count = HEAD_NUMBER * chain_count // res_ranks
    per_head = min(item_count, chain_count)
    head_count = item_count // per_head
    my_rank = lax.axis_index("res")
    my_group = lax.axis_index("seq")
    standardized_rows = layer_normalize(aligned_chain_embedding).astype(jnp.bfloat16)
    linear_mapped = jnp.dot(
        standardized_rows.reshape(chain_count * amino_count, ROW_FEATURES),
        combined_projection_matrix,
        preferred_element_type=jnp.float32,
    )
    linear_mapped = linear_mapped.reshape(chain_count, amino_count, 4, HEAD_NUMBER, PER_HEAD_DIM)
    queries = (linear_mapped[:, :, 0] * PER_HEAD_DIM ** (-0.5)).astype(jnp.bfloat16)
    key_rows = linear_mapped[:, :, 1].astype(jnp.bfloat16)
    value_rows = linear_mapped[:, :, 2].astype(jnp.bfloat16)
    sigmoid_factor = jax.nn.sigmoid(linear_mapped[:, :, 3])
    stacked = jnp.stack([queries, key_rows, value_rows], axis=2)
    stacked = jnp.transpose(stacked, (3, 0, 1, 2, 4)).reshape(
        HEAD_NUMBER * chain_count, amino_count, 3 * PER_HEAD_DIM
    )
    presence_mask_flags = alignment_mask.astype(jnp.bfloat16)
    key_flags = jnp.broadcast_to(
        presence_mask_flags[None], (HEAD_NUMBER, chain_count, amino_count)
    ).reshape(HEAD_NUMBER * chain_count, amino_count)
    arrived, arrived_flags = (
        lax.all_to_all(stacked, "res", split_axis=0, concat_axis=1, tiled=True),
        lax.all_to_all(key_flags, "res", split_axis=0, concat_axis=1, tiled=True),
    )
    pair_normed = layer_normalize(pairwise_state).astype(jnp.bfloat16)
    local_bias = jnp.dot(
        pair_normed.reshape(row_count * amino_count, CZ),
        pair_bias_weight,
        preferred_element_type=jnp.float32,
    )
    local_bias = jnp.transpose(
        local_bias.astype(jnp.bfloat16).reshape(row_count, amino_count, HEAD_NUMBER), (2, 0, 1)
    )
    bias_cols = lax.all_gather(local_bias, "res", axis=2, tiled=True)
    whole_bias = lax.all_gather(bias_cols, "seq", axis=1, tiled=True)
    first_head = my_rank * item_count // chain_count
    head_bias = lax.dynamic_slice_in_dim(whole_bias, first_head, head_count, 0)
    grouped = arrived.reshape(head_count, per_head, full_length, 3, PER_HEAD_DIM)
    key_validity_mask = (
        arrived_flags.reshape(head_count, per_head, full_length).astype(jnp.float32) - 1.0
    ) * 1000000000.0
    scores = jnp.einsum(
        "gpid,gpjd->gpij",
        grouped[:, :, :, 0],
        grouped[:, :, :, 1],
        preferred_element_type=jnp.float32,
    )
    scores = scores + head_bias.astype(jnp.float32)[:, None] + key_validity_mask[:, :, None, :]
    row_max = jnp.max(scores, axis=-1, keepdims=True)
    exponent = jnp.exp(scores - row_max)
    weights = (exponent / jnp.sum(exponent, axis=-1, keepdims=True)).astype(jnp.bfloat16)
    softmax_mixed = jnp.einsum(
        "gpij,gpjd->gpid", weights, grouped[:, :, :, 2], preferred_element_type=jnp.float32
    )
    softmax_mixed = softmax_mixed.astype(jnp.bfloat16).reshape(
        item_count, full_length, PER_HEAD_DIM
    )
    returned = lax.all_to_all(softmax_mixed, "res", split_axis=1, concat_axis=0, tiled=True)
    returned = jnp.transpose(
        returned.reshape(HEAD_NUMBER, chain_count, amino_count, PER_HEAD_DIM), (1, 2, 0, 3)
    )
    sigmoid_scaled = (
        (sigmoid_factor * returned.astype(jnp.float32))
        .astype(jnp.bfloat16)
        .reshape(chain_count * amino_count, ROW_FEATURES)
    )
    embedding_increment = jnp.dot(
        sigmoid_scaled, final_projection_matrix, preferred_element_type=jnp.float32
    ).reshape(chain_count, amino_count, ROW_FEATURES)
    alignment_output = (aligned_chain_embedding.astype(jnp.float32) + embedding_increment).astype(
        jnp.bfloat16
    )
    standardized_product = layer_normalize(alignment_output).astype(jnp.bfloat16)
    left_right_vectors = jnp.dot(
        standardized_product.reshape(chain_count * amino_count, ROW_FEATURES),
        left_right_projection_matrix,
        preferred_element_type=jnp.float32,
    )
    left_right_vectors = left_right_vectors.reshape(chain_count, amino_count, 2, PROJ_FEATURES)
    entry_present = alignment_mask.astype(jnp.float32)[:, :, None]
    left_side = (left_right_vectors[:, :, 0] * entry_present).astype(jnp.bfloat16)
    right_side = (left_right_vectors[:, :, 1] * entry_present).astype(jnp.bfloat16)
    left_all, left_flags = (
        lax.all_gather(left_side, "res", axis=1, tiled=True),
        lax.all_gather(presence_mask_flags, "res", axis=1, tiled=True),
    )
    project = outer_mean_weight.astype(jnp.float32)
    row_start = my_group * row_count
    left_full, flag_full = (
        lax.all_to_all(left_all, "seq", split_axis=1, concat_axis=0, tiled=True),
        lax.all_to_all(left_flags, "seq", split_axis=1, concat_axis=0, tiled=True),
    )
    right_full, right_flags = (
        lax.all_gather(right_side, "seq", axis=0, tiled=True),
        lax.all_gather(presence_mask_flags, "seq", axis=0, tiled=True),
    )
    counts = jnp.dot(flag_full.T, right_flags, preferred_element_type=jnp.float32)
    outer = outer_rows(left_full, right_full, project)
    col_start = my_rank * amino_count
    row_mask = lax.dynamic_slice_in_dim(resolved_residue_mask, row_start, row_count).astype(
        jnp.float32
    )
    col_mask = lax.dynamic_slice_in_dim(resolved_residue_mask, col_start, amino_count).astype(
        jnp.float32
    )
    pair_mask = row_mask[:, None] * col_mask[None, :]
    pairwise_output = (
        pairwise_state.astype(jnp.float32) + pair_mask[:, :, None] * (outer / counts[:, :, None])
    ).astype(jnp.bfloat16)
    return (alignment_output, pairwise_output)


def solution(mesh):
    placed = (
        P(("crop", "seq"), "res", None),
        P(("crop", "seq"), "res"),
        P("crop"),
        P(("crop", "seq"), "res", None),
        P(),
        P(),
        P(),
        P(),
        P(),
    )
    return jax.shard_map(
        per_device,
        mesh=mesh,
        in_specs=placed,
        out_specs=(P(("crop", "seq"), "res", None), P(("crop", "seq"), "res", None)),
        check_vma=False,
    )
```

profile of v0, /device:TPU:0, one launch (start us, length us, event | category | flops | bytes accessed | tf_op | source)
XLA Modules:
  0.0 115.8 jit_solution(7931450124926292603)
XLA Ops:
  0.6 0.8 fusion.49
  1.4 13.5 %all-gather = bf16[8,4,32]{2,1,0:T(4,128)(2,1)S(1)} all-gather(bf16[1,4,32]{2,1,0:T(4,128)(2,1)S(1)} %bitcast.150), channel_id=1, replica_groups=mesh['crop'=2,'seq'=2,'res'=8] {'res'}, dimensions={0}, use_global_device_ids=true | all-gather | bytes 2304 | tf_op jit(solution)/shard_map/all_gather | solution.py:146
  14.9 0.7 reshape.211
  15.5 3.2 %all-to-all-start.4 = ((bf16[2,2,256]{2,1,0:T(2,128)(2,1)}), bf16[2,2,256]{2,1,0:T(2,128)(2,1)S(1)}, u32[]{:S(2)}, u32[]{:S(2)}) async-start(bf16[2,2,256]{2,1,0:T(2,128)(2,1)} %reshape.211), calls=%async_computation.4 | async-start | bytes 4096 | tf_op jit(solution)/shard_map/all_to_all | solution.py:152
  18.8 1.2 %copy.71 = bf16[256,1024]{0,1:T(8,128)(2,1)S(1)} copy(bf16[256,1024]{1,0:T(8,128)(2,1)} %param.13) | data formatting | bytes 1048576 | tf_op args[4]
  20.0 0.9 convert_reduce_fusion
  21.0 1.0 fusion.21
  22.0 1.4 %fusion.30 = f32[32,4,4,8,32]{4,0,3,2,1:T(8,128)S(1)} fusion(bf16[4,8,32,256,1]{3,2,1,0,4:T(8,128)(2,1)S(1)} %bitcast.138, f32[32,4]{0,1:T(4,128)S(1)} %add_rsqrt_fusion.2, f32[32,4]{0,1:T(4,128)S(1)} %broadcast_multiply_fusion.3, bf16[32,4,256]{2,1,0:T(4,128)(2,1)} %param.9), kind=kOutput, calls=%fused_computation.47 | convolution fusion | flops 67239936 | bytes 1115136 | tf_op jit(solution)/shard_map/dot_general | solution.py:64
  23.7 0.2 fusion.44
  24.0 0.1 convolution_convert_fusion.1
  24.3 14.0 %all_gather.18 = bf16[8,16,32]{1,0,2:T(8,128)(2,1)S(1)} all-gather(bf16[8,16,4]{1,0,2:T(8,128)(2,1)S(1)} %copy.81), channel_id=1, replica_groups=mesh['crop'=2,'seq'=2,'res'=8] {'res'}, dimensions={2}, use_global_device_ids=true | all-gather | bytes 9216 | tf_op jit(solution)/shard_map/all_gather | solution.py:95
  38.5 4.6 %all_gather.19 = bf16[8,32,32]{2,0,1:T(8,128)(2,1)S(1)} all-gather(bf16[8,16,32]{2,0,1:T(8,128)(2,1)S(1)} %copy.82), channel_id=1, replica_groups=mesh['crop'=2,'seq'=2,'res'=8] {'seq'}, dimensions={1}, use_global_device_ids=true | all-gather | bytes 24576 | tf_op jit(solution)/shard_map/all_gather | solution.py:96
  43.1 1.0 maximum_bitcast_fusion
  44.2 0.6 broadcast_in_dim.4
  44.8 3.3 %all-to-all-start.1 = ((bf16[8,32,4]{1,2,0:T(4,128)(2,1)}), bf16[8,32,4]{1,2,0:T(4,128)(2,1)S(1)}, u32[]{:S(2)}, u32[]{:S(2)}) async-start(bf16[8,32,4]{1,2,0:T(4,128)(2,1)} %broadcast_in_dim.4), calls=%async_computation.1 | async-start | bytes 16384 | tf_op jit(solution)/shard_map/all_to_all | solution.py:84
  48.2 1.8 %copy.103 = bf16[8,32,4,3,32]{4,3,2,1,0:T(4,128)(2,1)S(1)} copy(bf16[8,32,4,3,32]{4,1,0,3,2:T(8,128)(2,1)} %maximum_bitcast_fusion) | data formatting | bytes 393216 | tf_op jit(solution)/shard_map/reshape | solution.py:75
  50.0 1.2 %reshape.205 = bf16[256,4,96]{2,1,0:T(4,128)(2,1)} reshape(bf16[8,32,4,3,32]{4,3,2,1,0:T(4,128)(2,1)S(1)} %copy.103) | data formatting | bytes 393216 | tf_op jit(solution)/shard_map/reshape | solution.py:75
  51.3 4.2 %all-gather.1 = bf16[2,32,4]{1,2,0:T(4,128)(2,1)S(1)} all-gather(bf16[1,32,4]{1,2,0:T(4,128)(2,1)S(1)} %bitcast.151), channel_id=1, replica_groups=mesh['crop'=2,'seq'=2,'res'=8] {'seq'}, dimensions={0}, use_global_device_ids=true | all-gather | bytes 768 | tf_op jit(solution)/shard_map/all_gather | solution.py:156
  55.6 5.0 %all-to-all-start = ((bf16[256,4,96]{2,1,0:T(4,128)(2,1)}), bf16[256,4,96]{2,1,0:T(4,128)(2,1)S(1)}, u32[]{:S(2)}, u32[]{:S(2)}) async-start(bf16[256,4,96]{2,1,0:T(4,128)(2,1)} %reshape.205), calls=%async_computation | async-start | bytes 524288 | tf_op jit(solution)/shard_map/all_to_all | solution.py:83
  60.9 9.5 %all-to-all-done = bf16[256,4,96]{2,1,0:T(4,128)(2,1)S(1)} async-done(((bf16[256,4,96]{2,1,0:T(4,128)(2,1)}), bf16[256,4,96]{2,1,0:T(4,128)(2,1)S(1)}, u32[]{:S(2)}, u32[]{:S(2)}) %all-to-all-start) | async-done | bytes 196640 | tf_op jit(solution)/shard_map/all_to_all | solution.py:83
  70.4 0.7 copy.75
  71.1 2.2 %reshape.185 = bf16[1,32,32,3,32]{4,3,1,2,0:T(4,128)(2,1)S(1)} reshape(bf16[32,8,4,96]{3,0,2,1:T(8,128)(2,1)} %copy.75) | data formatting | bytes 393216 | tf_op jit(solution)/shard_map/reshape | solution.py:99
  73.3 2.0 %fusion.48 = (bf16[1,32,32,1,32]{4,3,1,2,0:T(2,128)(2,1)S(1)}, bf16[1,32,32,1,32]{4,3,1,2,0:T(2,128)(2,1)S(1)}, bf16[1,32,32,1,32]{4,3,1,2,0:T(2,128)(2,1)}) fusion(bf16[1,32,32,3,32]{4,3,1,2,0:T(4,128)(2,1)S(1)} %reshape.185), kind=kLoop, calls=%fused_computation.80 | loop fusion | bytes 393216 | tf_op jit(solution)/shard_map/slice | solution.py:105
  75.3 0.7 fusion.3
  76.0 0.2 fusion.50
  76.2 1.5 %convolution_convert_fusion = bf16[32,32,32]{2,1,0:T(8,128)(2,1)S(1)} fusion(bf16[1,32,32,1,32]{4,3,1,2,0:T(2,128)(2,1)} %get-tuple-element.27, f32[32,32]{1,0:T(8,128)S(1)} %fusion.50, f32[32,32,32]{1,2,0:T(8,128)S(1)} %fusion.3), kind=kOutput, calls=%fused_computation.6 | convolution fusion | flops 2229279 | bytes 266240 | tf_op jit(solution)/shard_map/gpij,gpjd->gpid/dot_general | solution.py:113
  77.9 0.9 reshape.207
  78.8 3.4 %all-to-all-start.2 = ((bf16[8,2,2048]{2,1,0:T(2,128)(2,1)}), bf16[8,2,2048]{2,1,0:T(2,128)(2,1)S(1)}, u32[]{:S(2)}, u32[]{:S(2)}) async-start(bf16[8,2,2048]{2,1,0:T(2,128)(2,1)} %reshape.207), calls=%async_computation.2 | async-start | bytes 131072 | tf_op jit(solution)/shard_map/all_to_all | solution.py:119
  82.2 5.7 %all-to-all-done.2 = bf16[8,2,2048]{2,1,0:T(2,128)(2,1)S(1)} async-done(((bf16[8,2,2048]{2,1,0:T(2,128)(2,1)}), bf16[8,2,2048]{2,1,0:T(2,128)(2,1)S(1)}, u32[]{:S(2)}, u32[]{:S(2)}) %all-to-all-start.2) | async-done | bytes 65568 | tf_op jit(solution)/shard_map/all_to_all | solution.py:119
  88.0 0.2 reshape.208
  88.2 0.1 fusion.14
  88.4 0.2 dot_general.47
  88.6 0.2 convert_reduce_fusion.1
  88.9 0.2 fusion.23
  89.1 0.2 fusion.27
  89.4 14.2 %all_gather.21 = bf16[32,32,32]{2,0,1:T(8,128)(2,1)S(1)} all-gather(bf16[32,4,32]{2,0,1:T(8,128)(2,1)S(1)} %get-tuple-element.29), channel_id=1, replica_groups=mesh['crop'=2,'seq'=2,'res'=8] {'res'}, dimensions={1}, use_global_device_ids=true | all-gather | bytes 73728 | tf_op jit(solution)/shard_map/all_gather | solution.py:145
  103.6 0.9 reshape.209
  104.5 3.3 %all-to-all-start.3 = ((bf16[2,2,8192]{2,1,0:T(2,128)(2,1)}), bf16[2,2,8192]{2,1,0:T(2,128)(2,1)S(1)}, u32[]{:S(2)}, u32[]{:S(2)}) async-start(bf16[2,2,8192]{2,1,0:T(2,128)(2,1)} %reshape.209), calls=%async_computation.3 | async-start | bytes 131072 | tf_op jit(solution)/shard_map/all_to_all | solution.py:151
  107.9 0.7 copy.97
  108.6 4.6 %all_gather.20 = bf16[64,4,32]{2,0,1:T(8,128)(2,1)S(1)} all-gather(bf16[32,4,32]{2,0,1:T(8,128)(2,1)S(1)} %get-tuple-element.28), channel_id=1, replica_groups=mesh['crop'=2,'seq'=2,'res'=8] {'seq'}, dimensions={0}, use_global_device_ids=true | all-gather | bytes 24576 | tf_op jit(solution)/shard_map/all_gather | solution.py:155
  113.2 0.2 reshape.210
  113.4 0.2 copy.92
  113.6 0.1 reshape.203
  113.7 0.4 convolution_bitcast_fusion
  114.1 0.3 copy.94
  114.4 0.5 dot_general.53
  114.9 0.3 fusion.7
  115.2 0.6 copy.98
  (50 shorter events, 1.9 us)
Async XLA Ops:
  0.6 114.3 %copy-start = (bf16[1024,128]{1,0:T(8,128)(2,1)S(1)}, bf16[1024,128]{1,0:T(8,128)(2,1)}, u32[]{:S(2)}) copy-start(bf16[1024,128]{1,0:T(8,128)(2,1)} %param.17) | copy-start | bytes 786436
  15.5 28.7 %all-to-all-start.4 = ((bf16[2,2,256]{2,1,0:T(2,128)(2,1)}), bf16[2,2,256]{2,1,0:T(2,128)(2,1)S(1)}, u32[]{:S(2)}, u32[]{:S(2)}) async-start(bf16[2,2,256]{2,1,0:T(2,128)(2,1)} %reshape.211), calls=%async_computation.4 | async-start | bytes 4096 | tf_op jit(solution)/shard_map/all_to_all | solution.py:152
  22.0 1.6 %copy-start.2 = (bf16[16,4,128]{2,1,0:T(4,128)(2,1)S(1)}, bf16[16,4,128]{2,1,0:T(4,128)(2,1)}, u32[]{:S(2)}) copy-start(bf16[16,4,128]{2,1,0:T(4,128)(2,1)} %param.12) | copy-start | bytes 49156
  22.0 2.0 %copy-start.5 = (bf16[128,8]{0,1:T(8,128)(2,1)S(1)}, bf16[128,8]{0,1:T(8,128)(2,1)}, u32[]{:S(2)}) copy-start(bf16[128,8]{0,1:T(8,128)(2,1)} %param.14) | copy-start | bytes 6148
  23.4 20.7 %copy-start.6 = (s32[32]{0:T(128)S(1)}, s32[32]{0:T(128)}, u32[]{:S(2)}) copy-start(s32[32]{0:T(128)} %param.11) | copy-start | bytes 388
  44.8 10.8 %all-to-all-start.1 = ((bf16[8,32,4]{1,2,0:T(4,128)(2,1)}), bf16[8,32,4]{1,2,0:T(4,128)(2,1)S(1)}, u32[]{:S(2)}, u32[]{:S(2)}) async-start(bf16[8,32,4]{1,2,0:T(4,128)(2,1)} %broadcast_in_dim.4), calls=%async_computation.1 | async-start | bytes 16384 | tf_op jit(solution)/shard_map/all_to_all | solution.py:84
  55.6 14.7 %all-to-all-start = ((bf16[256,4,96]{2,1,0:T(4,128)(2,1)}), bf16[256,4,96]{2,1,0:T(4,128)(2,1)S(1)}, u32[]{:S(2)}, u32[]{:S(2)}) async-start(bf16[256,4,96]{2,1,0:T(4,128)(2,1)} %reshape.205), calls=%async_computation | async-start | bytes 524288 | tf_op jit(solution)/shard_map/all_to_all | solution.py:83
  77.7 10.9 %copy-start.1 = (bf16[32,4,256]{2,1,0:T(4,128)(2,1)S(1)}, bf16[32,4,256]{2,1,0:T(4,128)(2,1)}, u32[]{:S(2)}) copy-start(bf16[32,4,256]{2,1,0:T(4,128)(2,1)} %param.9) | copy-start | bytes 196612
  77.7 10.9 %copy-start.3 = (bf16[256,256]{1,0:T(8,128)(2,1)S(1)}, bf16[256,256]{1,0:T(8,128)(2,1)}, u32[]{:S(2)}) copy-start(bf16[256,256]{1,0:T(8,128)(2,1)} %param.15) | copy-start | bytes 393220
  77.7 11.4 %copy-start.4 = (bf16[256,64]{0,1:T(8,128)(2,1)S(1)}, bf16[256,64]{0,1:T(8,128)(2,1)}, u32[]{:S(2)}) copy-start(bf16[256,64]{0,1:T(8,128)(2,1)} %param.16) | copy-start | bytes 98308
  78.8 9.2 %all-to-all-start.2 = ((bf16[8,2,2048]{2,1,0:T(2,128)(2,1)}), bf16[8,2,2048]{2,1,0:T(2,128)(2,1)S(1)}, u32[]{:S(2)}, u32[]{:S(2)}) async-start(bf16[8,2,2048]{2,1,0:T(2,128)(2,1)} %reshape.207), calls=%async_computation.2 | async-start | bytes 131072 | tf_op jit(solution)/shard_map/all_to_all | solution.py:119
  104.5 8.7 %all-to-all-start.3 = ((bf16[2,2,8192]{2,1,0:T(2,128)(2,1)}), bf16[2,2,8192]{2,1,0:T(2,128)(2,1)S(1)}, u32[]{:S(2)}, u32[]{:S(2)}) async-start(bf16[2,2,8192]{2,1,0:T(2,128)(2,1)} %reshape.209), calls=%async_computation.3 | async-start | bytes 131072 | tf_op jit(solution)/shard_map/all_to_all | solution.py:151
where the time goes:
time: 117 us; the launch traced here: 116 us
  blocking collectives  55 us (47%)
  starting transfers between devices  18.2 us (16%)
  local copies, waits for them, and re-layouts  16.4 us (14%)
  waiting for transfers between devices  15.2 us (13%)
  matrix products  4.99 us (4%)
  other arithmetic  4.97 us (4%)
    all_gather x1, blocking collectives, per_device(): lax.all_gather(left_side, 'res', axis=1, tiled=True)  14.2 us
    all_gather x1, blocking collectives, per_device(): bias_cols = lax.all_gather(local_bias, 'res', axis=2, tiled=True)  14 us
    all_gather x1, blocking collectives, per_device(): lax.all_gather(presence_mask_flags, 'res', axis=1, tiled=True)  13.5 us
    all_to_all x1, waiting for transfers between devices, per_device(): lax.all_to_all(stacked, 'res', split_axis=0, concat_axis=1, tiled=True)  9.47 us
    all_to_all x1, waiting for transfers between devices, per_device(): lax.all_to_all(softmax_mixed, 'res', split_axis=1, concat_axis=0, tiled=T...  5.73 us
    unnamed x24, local copies, waits for them, and re-layouts  5.6 us
    all_to_all x1, starting transfers between devices, per_device(): lax.all_to_all(stacked, 'res', split_axis=0, concat_axis=1, tiled=True)  5.02 us
    all_gather x1, blocking collectives, per_device(): whole_bias = lax.all_gather(bias_cols, 'seq', axis=1, tiled=True)  4.58 us
  transfers between devices with their start and end apart: 5, of which 2 were waited for; matrix products, arithmetic and copies ran while one was open for 9% of the time, Pallas kernels for 0%

commit v1 on v0

--- a/solution.py
+++ b/solution.py
@@ -1,3 +1,4 @@
+import functools
 import math
 import jax
 import jax.numpy as jnp
@@ -10,6 +11,14 @@
 PER_HEAD_DIM = 32
 PROJ_FEATURES = 32
 epsilon = 1e-05
+
+
+def close_the_words(body, dim_at):
+    r_now = lax.all_gather(body, "res")
+    return jnp.concatenate(r_now, dim_at)
+
+
+loops_choose = functools.partial(close_the_words, dim_at=1)
 
 
 def layer_normalize(values):
@@ -142,7 +151,7 @@
     left_side = (left_right_vectors[:, :, 0] * entry_present).astype(jnp.bfloat16)
     right_side = (left_right_vectors[:, :, 1] * entry_present).astype(jnp.bfloat16)
     left_all, left_flags = (
-        lax.all_gather(left_side, "res", axis=1, tiled=True),
+        loops_choose(left_side),
         lax.all_gather(presence_mask_flags, "res", axis=1, tiled=True),
     )
     project = outer_mean_weight.astype(jnp.float32)

time: 117 us -> 115 us (0.983)
  local copies, waits for them, and re-layouts: 16.4 us -> 15.2 us
  transfers between devices with their start and end apart: 5 -> 5, of which waited for: 2 -> 2; matrix products, arithmetic and copies ran while one was open for 9% -> 8% of each run, Pallas kernels for 0% -> 0%
where the time goes in v1:
time: 115 us; the launch traced here: 114 us
  blocking collectives  55.1 us (48%)
  starting transfers between devices  18.2 us (16%)
  waiting for transfers between devices  15.3 us (13%)
  local copies, waits for them, and re-layouts  15.2 us (13%)
  matrix products  4.97 us (4%)
  other arithmetic  4.18 us (4%)
    all_gather x1, blocking collectives, close_the_words(): r_now = lax.all_gather(body, 'res')  14.2 us
    all_gather x1, blocking collectives, per_device(): bias_cols = lax.all_gather(local_bias, 'res', axis=2, tiled=True)  14 us
    all_gather x1, blocking collectives, per_device(): lax.all_gather(presence_mask_flags, 'res', axis=1, tiled=True)  13.5 us
    all_to_all x1, waiting for transfers between devices, per_device(): lax.all_to_all(stacked, 'res', split_axis=0, concat_axis=1, tiled=True)  9.52 us
    all_to_all x1, waiting for transfers between devices, per_device(): lax.all_to_all(softmax_mixed, 'res', split_axis=1, concat_axis=0, tiled=T...  5.73 us
    unnamed x24, local copies, waits for them, and re-layouts  5.61 us
    all_to_all x1, starting transfers between devices, per_device(): lax.all_to_all(stacked, 'res', split_axis=0, concat_axis=1, tiled=True)  5.03 us
    all_gather x1, blocking collectives, per_device(): whole_bias = lax.all_gather(bias_cols, 'seq', axis=1, tiled=True)  4.58 us
  transfers between devices with their start and end apart: 5, of which 2 were waited for; matrix products, arithmetic and copies ran while one was open for 8% of the time, Pallas kernels for 0%

profile of v1, /device:TPU:0, one launch (start us, length us, event | category | flops | bytes accessed | tf_op | source)
XLA Modules:
  0.0 114.0 jit_solution(12454419415420637431)
XLA Ops:
  0.6 0.8 fusion.49
  1.4 13.5 %all-gather = bf16[8,4,32]{2,1,0:T(4,128)(2,1)S(1)} all-gather(bf16[1,4,32]{2,1,0:T(4,128)(2,1)S(1)} %bitcast.151), channel_id=1, replica_groups=mesh['crop'=2,'seq'=2,'res'=8] {'res'}, dimensions={0}, use_global_device_ids=true | all-gather | bytes 2304 | tf_op jit(solution)/shard_map/all_gather | solution.py:155
  14.9 0.7 reshape.232
  15.5 3.2 %all-to-all-start.4 = ((bf16[2,2,256]{2,1,0:T(2,128)(2,1)}), bf16[2,2,256]{2,1,0:T(2,128)(2,1)S(1)}, u32[]{:S(2)}, u32[]{:S(2)}) async-start(bf16[2,2,256]{2,1,0:T(2,128)(2,1)} %reshape.232), calls=%async_computation.4 | async-start | bytes 4096 | tf_op jit(solution)/shard_map/all_to_all | solution.py:161
  18.8 1.2 %copy.124 = bf16[256,1024]{0,1:T(8,128)(2,1)S(1)} copy(bf16[256,1024]{1,0:T(8,128)(2,1)} %param.13) | data formatting | bytes 1048576 | tf_op args[4]
  20.1 0.9 convert_reduce_fusion
  21.0 1.0 fusion.21
  22.0 1.4 %fusion.30 = f32[32,4,4,8,32]{4,0,3,2,1:T(8,128)S(1)} fusion(bf16[4,8,32,256,1]{3,2,1,0,4:T(8,128)(2,1)S(1)} %bitcast.140, f32[32,4]{0,1:T(4,128)S(1)} %add_rsqrt_fusion.2, f32[32,4]{0,1:T(4,128)S(1)} %broadcast_multiply_fusion.3, bf16[32,4,256]{2,1,0:T(4,128)(2,1)} %param.9), kind=kOutput, calls=%fused_computation.47 | convolution fusion | flops 67239936 | bytes 1115136 | tf_op jit(solution)/shard_map/dot_general | solution.py:73
  23.6 0.2 fusion.44
  23.9 0.1 convolution_convert_fusion.1
  24.3 14.0 %all_gather.19 = bf16[8,16,32]{1,0,2:T(8,128)(2,1)S(1)} all-gather(bf16[8,16,4]{1,0,2:T(8,128)(2,1)S(1)} %copy.134), channel_id=1, replica_groups=mesh['crop'=2,'seq'=2,'res'=8] {'res'}, dimensions={2}, use_global_device_ids=true | all-gather | bytes 9216 | tf_op jit(solution)/shard_map/all_gather | solution.py:104
  38.4 4.6 %all_gather.20 = bf16[8,32,32]{2,0,1:T(8,128)(2,1)S(1)} all-gather(bf16[8,16,32]{2,0,1:T(8,128)(2,1)S(1)} %copy.135), channel_id=1, replica_groups=mesh['crop'=2,'seq'=2,'res'=8] {'seq'}, dimensions={1}, use_global_device_ids=true | all-gather | bytes 24576 | tf_op jit(solution)/shard_map/all_gather | solution.py:105
  43.3 0.6 broadcast_in_dim.4
  43.9 3.3 %all-to-all-start.1 = ((bf16[8,32,4]{1,2,0:T(4,128)(2,1)}), bf16[8,32,4]{1,2,0:T(4,128)(2,1)S(1)}, u32[]{:S(2)}, u32[]{:S(2)}) async-start(bf16[8,32,4]{1,2,0:T(4,128)(2,1)} %broadcast_in_dim.4), calls=%async_computation.1 | async-start | bytes 16384 | tf_op jit(solution)/shard_map/all_to_all | solution.py:93
  47.3 0.2 maximum_bitcast_fusion
  47.4 0.7 copy.156
  48.1 1.2 %reshape.226 = bf16[256,4,96]{2,1,0:T(4,128)(2,1)} reshape(bf16[8,32,4,3,32]{4,3,2,1,0:T(4,128)(2,1)S(1)} %copy.156) | data formatting | bytes 393216 | tf_op jit(solution)/shard_map/reshape | solution.py:84
  49.4 4.2 %all-gather.1 = bf16[2,32,4]{1,2,0:T(4,128)(2,1)S(1)} all-gather(bf16[1,32,4]{1,2,0:T(4,128)(2,1)S(1)} %bitcast.152), channel_id=1, replica_groups=mesh['crop'=2,'seq'=2,'res'=8] {'seq'}, dimensions={0}, use_global_device_ids=true | all-gather | bytes 768 | tf_op jit(solution)/shard_map/all_gather | solution.py:165
  53.8 5.0 %all-to-all-start = ((bf16[256,4,96]{2,1,0:T(4,128)(2,1)}), bf16[256,4,96]{2,1,0:T(4,128)(2,1)S(1)}, u32[]{:S(2)}, u32[]{:S(2)}) async-start(bf16[256,4,96]{2,1,0:T(4,128)(2,1)} %reshape.226), calls=%async_computation | async-start | bytes 524288 | tf_op jit(solution)/shard_map/all_to_all | solution.py:92
  59.0 9.5 %all-to-all-done = bf16[256,4,96]{2,1,0:T(4,128)(2,1)S(1)} async-done(((bf16[256,4,96]{2,1,0:T(4,128)(2,1)}), bf16[256,4,96]{2,1,0:T(4,128)(2,1)S(1)}, u32[]{:S(2)}, u32[]{:S(2)}) %all-to-all-start) | async-done | bytes 196640 | tf_op jit(solution)/shard_map/all_to_all | solution.py:92
  68.6 0.7 copy.128
  69.3 2.2 %reshape.204 = bf16[1,32,32,3,32]{4,3,1,2,0:T(4,128)(2,1)S(1)} reshape(bf16[32,8,4,96]{3,0,2,1:T(8,128)(2,1)} %copy.128) | data formatting | bytes 393216 | tf_op jit(solution)/shard_map/reshape | solution.py:108
  71.5 2.0 %fusion.48 = (bf16[1,32,32,1,32]{4,3,1,2,0:T(2,128)(2,1)S(1)}, bf16[1,32,32,1,32]{4,3,1,2,0:T(2,128)(2,1)S(1)}, bf16[1,32,32,1,32]{4,3,1,2,0:T(2,128)(2,1)}) fusion(bf16[1,32,32,3,32]{4,3,1,2,0:T(4,128)(2,1)S(1)} %reshape.204), kind=kLoop, calls=%fused_computation.80 | loop fusion | bytes 393216 | tf_op jit(solution)/shard_map/slice | solution.py:114
  73.5 0.7 fusion.3
  74.2 0.2 fusion.50
  74.3 1.5 %convolution_convert_fusion = bf16[32,32,32]{2,1,0:T(8,128)(2,1)S(1)} fusion(bf16[1,32,32,1,32]{4,3,1,2,0:T(2,128)(2,1)} %get-tuple-element.31, f32[32,32]{1,0:T(8,128)S(1)} %fusion.50, f32[32,32,32]{1,2,0:T(8,128)S(1)} %fusion.3), kind=kOutput, calls=%fused_computation.6 | convolution fusion | flops 2229279 | bytes 266240 | tf_op jit(solution)/shard_map/gpij,gpjd->gpid/dot_general | solution.py:122
  76.0 0.9 reshape.228
  77.0 3.4 %all-to-all-start.2 = ((bf16[8,2,2048]{2,1,0:T(2,128)(2,1)}), bf16[8,2,2048]{2,1,0:T(2,128)(2,1)S(1)}, u32[]{:S(2)}, u32[]{:S(2)}) async-start(bf16[8,2,2048]{2,1,0:T(2,128)(2,1)} %reshape.228), calls=%async_computation.2 | async-start | bytes 131072 | tf_op jit(solution)/shard_map/all_to_all | solution.py:128
  80.4 5.7 %all-to-all-done.2 = bf16[8,2,2048]{2,1,0:T(2,128)(2,1)S(1)} async-done(((bf16[8,2,2048]{2,1,0:T(2,128)(2,1)}), bf16[8,2,2048]{2,1,0:T(2,128)(2,1)S(1)}, u32[]{:S(2)}, u32[]{:S(2)}) %all-to-all-start.2) | async-done | bytes 65568 | tf_op jit(solution)/shard_map/all_to_all | solution.py:128
  86.2 0.2 reshape.229
  86.4 0.1 fusion.14
  86.6 0.2 dot_general.47
  86.8 0.3 convert_reduce_fusion.1
  87.1 0.2 fusion.23
  87.3 0.2 fusion.27
  87.6 14.2 %all_gather.22 = bf16[8,32,4,32]{3,1,2,0:T(8,128)(2,1)S(1)} all-gather(bf16[1,32,4,32]{3,1,2,0:T(8,128)(2,1)S(1)} %fusion.33), channel_id=1, replica_groups=mesh['crop'=2,'seq'=2,'res'=8] {'res'}, dimensions={0}, use_global_device_ids=true | all-gather | bytes 73728 | tf_op jit(solution)/shard_map/all_gather | solution.py:17
  101.8 0.9 reshape.230
  102.7 3.3 %all-to-all-start.3 = ((bf16[2,2,8192]{2,1,0:T(2,128)(2,1)}), bf16[2,2,8192]{2,1,0:T(2,128)(2,1)S(1)}, u32[]{:S(2)}, u32[]{:S(2)}) async-start(bf16[2,2,8192]{2,1,0:T(2,128)(2,1)} %reshape.230), calls=%async_computation.3 | async-start | bytes 131072 | tf_op jit(solution)/shard_map/all_to_all | solution.py:160
  106.1 0.7 copy.150
  106.8 4.6 %all_gather.21 = bf16[64,4,32]{2,0,1:T(8,128)(2,1)S(1)} all-gather(bf16[32,4,32]{2,0,1:T(8,128)(2,1)S(1)} %fusion.35), channel_id=1, replica_groups=mesh['crop'=2,'seq'=2,'res'=8] {'seq'}, dimensions={0}, use_global_device_ids=true | all-gather | bytes 24576 | tf_op jit(solution)/shard_map/all_gather | solution.py:164
  111.4 0.2 reshape.231
  111.6 0.2 copy.145
  111.8 0.1 reshape.224
  111.9 0.4 convolution_bitcast_fusion
  112.3 0.3 copy.147
  112.6 0.5 dot_general.53
  113.1 0.3 fusion.7
  113.4 0.6 copy.151
  (51 shorter events, 1.9 us)
Async XLA Ops:
  0.6 112.5 %copy-start = (bf16[1024,128]{1,0:T(8,128)(2,1)S(1)}, bf16[1024,128]{1,0:T(8,128)(2,1)}, u32[]{:S(2)}) copy-start(bf16[1024,128]{1,0:T(8,128)(2,1)} %param.17) | copy-start | bytes 786436
  15.5 27.8 %all-to-all-start.4 = ((bf16[2,2,256]{2,1,0:T(2,128)(2,1)}), bf16[2,2,256]{2,1,0:T(2,128)(2,1)S(1)}, u32[]{:S(2)}, u32[]{:S(2)}) async-start(bf16[2,2,256]{2,1,0:T(2,128)(2,1)} %reshape.232), calls=%async_computation.4 | async-start | bytes 4096 | tf_op jit(solution)/shard_map/all_to_all | solution.py:161
  18.8 4.8 %copy-start.2 = (bf16[16,4,128]{2,1,0:T(4,128)(2,1)S(1)}, bf16[16,4,128]{2,1,0:T(4,128)(2,1)}, u32[]{:S(2)}) copy-start(bf16[16,4,128]{2,1,0:T(4,128)(2,1)} %param.12) | copy-start | bytes 49156
  20.0 3.9 %copy-start.5 = (bf16[128,8]{0,1:T(8,128)(2,1)S(1)}, bf16[128,8]{0,1:T(8,128)(2,1)}, u32[]{:S(2)}) copy-start(bf16[128,8]{0,1:T(8,128)(2,1)} %param.14) | copy-start | bytes 6148
  20.0 22.9 %copy-start.6 = (s32[32]{0:T(128)S(1)}, s32[32]{0:T(128)}, u32[]{:S(2)}) copy-start(s32[32]{0:T(128)} %param.11) | copy-start | bytes 388
  43.9 9.8 %all-to-all-start.1 = ((bf16[8,32,4]{1,2,0:T(4,128)(2,1)}), bf16[8,32,4]{1,2,0:T(4,128)(2,1)S(1)}, u32[]{:S(2)}, u32[]{:S(2)}) async-start(bf16[8,32,4]{1,2,0:T(4,128)(2,1)} %broadcast_in_dim.4), calls=%async_computation.1 | async-start | bytes 16384 | tf_op jit(solution)/shard_map/all_to_all | solution.py:93
  53.8 14.7 %all-to-all-start = ((bf16[256,4,96]{2,1,0:T(4,128)(2,1)}), bf16[256,4,96]{2,1,0:T(4,128)(2,1)S(1)}, u32[]{:S(2)}, u32[]{:S(2)}) async-start(bf16[256,4,96]{2,1,0:T(4,128)(2,1)} %reshape.226), calls=%async_computation | async-start | bytes 524288 | tf_op jit(solution)/shard_map/all_to_all | solution.py:92
  75.9 10.9 %copy-start.1 = (bf16[32,4,256]{2,1,0:T(4,128)(2,1)S(1)}, bf16[32,4,256]{2,1,0:T(4,128)(2,1)}, u32[]{:S(2)}) copy-start(bf16[32,4,256]{2,1,0:T(4,128)(2,1)} %param.9) | copy-start | bytes 196612
  75.9 10.9 %copy-start.3 = (bf16[256,256]{1,0:T(8,128)(2,1)S(1)}, bf16[256,256]{1,0:T(8,128)(2,1)}, u32[]{:S(2)}) copy-start(bf16[256,256]{1,0:T(8,128)(2,1)} %param.15) | copy-start | bytes 393220
  75.9 11.4 %copy-start.4 = (bf16[256,64]{0,1:T(8,128)(2,1)S(1)}, bf16[256,64]{0,1:T(8,128)(2,1)}, u32[]{:S(2)}) copy-start(bf16[256,64]{0,1:T(8,128)(2,1)} %param.16) | copy-start | bytes 98308
  77.0 9.2 %all-to-all-start.2 = ((bf16[8,2,2048]{2,1,0:T(2,128)(2,1)}), bf16[8,2,2048]{2,1,0:T(2,128)(2,1)S(1)}, u32[]{:S(2)}, u32[]{:S(2)}) async-start(bf16[8,2,2048]{2,1,0:T(2,128)(2,1)} %reshape.228), calls=%async_computation.2 | async-start | bytes 131072 | tf_op jit(solution)/shard_map/all_to_all | solution.py:128
  102.7 8.6 %all-to-all-start.3 = ((bf16[2,2,8192]{2,1,0:T(2,128)(2,1)}), bf16[2,2,8192]{2,1,0:T(2,128)(2,1)S(1)}, u32[]{:S(2)}, u32[]{:S(2)}) async-start(bf16[2,2,8192]{2,1,0:T(2,128)(2,1)} %reshape.230), calls=%async_computation.3 | async-start | bytes 131072 | tf_op jit(solution)/shard_map/all_to_all | solution.py:160
